TPU v7x, 32 devices: a whole 2x2x4 slice. The times are simulated.
32 devices in a mesh: fsdp: 4 (over z), tp: 4 (over y, x), job: 2 (over core).
Axes of the slice: x: 2, y: 2, z: 4, core: 2. Of those that a mesh axis runs over, the one named last changes fastest.
Arguments:
- slopes_in: float32 [128, 128, 1024], P('job', 'fsdp', 'tp'), parts along dimension 0, may hold values from -6 to 6
- moments_in: float32 [128, 128, 1024], P('job', 'fsdp', 'tp'), parts along dimension 0, may hold values from -6 to 6
- weights_in: float32 [128, 128, 1024], P('job', 'fsdp', 'tp'), parts along dimension 0, may hold values from -0.1875 to 0.1875
Outputs:
- new_weights: float32 [128, 128, 1024], P('job', 'fsdp', 'tp'), parts along dimension 0
- new_momentum: float32 [128, 128, 1024], P('job', 'fsdp', 'tp'), parts along dimension 0
There are 2 independent parts, one for each index of `job`. A program takes and returns all parts, laid end to end along the dimension named above; each array names one. Nothing has to cross between parts.
All inputs are finite; a program needn't handle non-finite values.
Results may differ from a plain program's by a relative error of at most 0.00019.
Values sent between devices are 32-bit elements; how exact they have to be, the bound alone decides.
A program may use at most 128 MiB of HBM per device.

v0:
```python
import functools

import jax
import jax.numpy as jnp
from jax import lax
from jax.experimental import pallas as pl
from jax.experimental.pallas import tpu as pltpu
from jax.sharding import PartitionSpec as P

ITERS = 5


hold_rate = 0.9
learn_rate = 0.8

COEF_A, COEF_B, COEF_C = 3.4445, -4.775, 2.0315
MESH = pl.DeviceIdType.MESH
HIGHEST = lax.Precision.HIGHEST


def dot(a, b, contract=((1,), (0,))):
    return lax.dot_general(
        a, b, (contract, ((), ())), precision=HIGHEST, preferred_element_type=jnp.float32
    )


def factor_of(gram):
    side = gram.shape[0]
    rows = lax.broadcasted_iota(jnp.int32, (side, side), 0)
    eye = rows == lax.broadcasted_iota(jnp.int32, (side, side), 1)
    total = jnp.sum(jnp.where(eye, gram, 0.0), axis=(0, 1), keepdims=True)
    scale = lax.rsqrt(total + 1e-06)

    def mixed_of(a):
        return COEF_B * a + COEF_C * dot(a, a)

    def step(_, carry):
        a, q = carry
        mixed = mixed_of(a)
        half = COEF_A * a + dot(mixed, a)
        return COEF_A * half + dot(half, mixed), COEF_A * q + dot(mixed, q)

    a = gram * scale * scale
    q = jnp.where(eye, jnp.broadcast_to(scale, gram.shape), 0.0)
    a, q = lax.fori_loop(0, ITERS - 1, step, (a, q))
    return COEF_A * q + dot(mixed_of(a), q)


def kernel(nf, nt, chunks, slopes, moments, weights, new, mom, out, wbuf, sbuf, mbuf, xbuf, gsend, grecv, qrecv, ybuf, fsend, frecv, gs, gr, qs, qr, bsend, brecv, own, loads):
    me_f, me_t = lax.axis_index("fsdp"), lax.axis_index("tp")
    mats, rows, _ = mom.shape
    share = mats // nf
    per = share // chunks
    each = per // nt

    barrier = pltpu.get_barrier_semaphore()
    for d in range(1, nf):
        pl.semaphore_signal(barrier, inc=1, device_id={"fsdp": lax.rem(me_f + d, nf)}, device_id_type=MESH)
    for d in range(1, nt):
        pl.semaphore_signal(barrier, inc=1, device_id={"tp": lax.rem(me_t + d, nt)}, device_id_type=MESH)

    order = [(c, d) for c in range(chunks) for d in list(range(1, nf)) + [0]]

    def block(c, d):
        return pl.ds(lax.rem(me_f + d, nf) * share + c * per, per)

    def load(c, d):
        here = block(c, d)
        return (
            pltpu.make_async_copy(slopes.at[here], sbuf.at[here], loads.at[0, c, d]),
            pltpu.make_async_copy(moments.at[here], mbuf.at[here], loads.at[1, c, d]),
        )

    for c, d in order:
        for copy in load(c, d):
            copy.start()
    fetch = pltpu.make_async_copy(weights, wbuf, own.at[2, 0])
    fetch.start()

    my_rows = pl.ds(pl.multiple_of(me_f * rows, rows), rows)

    def there(c, d):
        peer = lax.rem(me_f + d, nf)
        return pltpu.make_async_remote_copy(
            src_ref=mom.at[pl.ds(peer * share + c * per, per)],
            dst_ref=xbuf.at[pl.ds(c * per, per), my_rows, :],
            send_sem=fsend.at[c, d - 1], recv_sem=frecv.at[c, d - 1],
            device_id={"fsdp": peer}, device_id_type=MESH,
        )

    def stay(c):
        return pltpu.make_async_copy(
            mom.at[pl.ds(me_f * share + c * per, per)],
            xbuf.at[pl.ds(c * per, per), my_rows, :], own.at[0, c],
        )

    def back(c, d):
        peer = lax.rem(me_f + d, nf)
        theirs = pl.ds(pl.multiple_of(peer * rows, rows), rows)
        return pltpu.make_async_remote_copy(
            src_ref=ybuf.at[pl.ds(c * per, per), theirs, :],
            dst_ref=out.at[pl.ds(me_f * share + c * per, per)],
            send_sem=bsend.at[c, d - 1], recv_sem=brecv.at[c, d - 1],
            device_id={"fsdp": peer}, device_id_type=MESH,
        )

    def keep(c):
        return pltpu.make_async_copy(
            ybuf.at[pl.ds(c * per, per), my_rows, :],
            out.at[pl.ds(me_f * share + c * per, per)], own.at[1, c],
        )

    def gram_copy(c, d):
        return pltpu.make_async_remote_copy(
            src_ref=gsend.at[c, d - 1], dst_ref=grecv.at[c, d],
            send_sem=gs.at[c, d - 1], recv_sem=gr.at[c, d - 1],
            device_id={"tp": lax.rem(me_t + d, nt)}, device_id_type=MESH,
        )

    def factor_copy(c, d):
        return pltpu.make_async_remote_copy(
            src_ref=qrecv.at[c, 0], dst_ref=qrecv.at[c, d],
            send_sem=qs.at[c, d - 1], recv_sem=qr.at[c, d - 1],
            device_id={"tp": lax.rem(me_t + d, nt)}, device_id_type=MESH,
        )

    def grams(c):
        stay(c).wait()
        for d in range(1, nf):
            there(c, d).wait_recv()
        for d in list(range(1, nt)) + [0]:
            first = c * per + lax.rem(me_t + d, nt) * each
            for e in range(each):
                x = xbuf[first + e]
                g = dot(x, x, ((1,), (1,)))
                if d == 0:
                    grecv[c, 0, e] = g
                else:
                    gsend[c, d - 1, e] = g
            if d > 0:
                gram_copy(c, d).start()

    def factors(c):
        for d in range(1, nt):
            gram_copy(c, d).wait_recv()
        for e in range(each):
            g = grecv[c, 0, e]
            for d in range(1, nt):
                g = g + grecv[c, d, e]
            qrecv[c, 0, e] = factor_of(g)
        for d in range(1, nt):
            factor_copy(c, d).start()

    def apply(c):
        for d in range(nt):
            if d > 0:
                factor_copy(c, d).wait_recv()
            first = c * per + lax.rem(me_t - d + nt, nt) * each
            for e in range(each):
                ybuf[first + e] = dot(qrecv[c, d, e], xbuf[first + e])
        for d in range(1, nf):
            back(c, d).start()
        keep(c).start()

    def send(c, d):
        if d > 0:
            there(c, d).start()
        else:
            stay(c).start()

    def momentum(c, d):
        for copy in load(c, d):
            copy.wait()
        here = block(c, d)
        mom[here] = hold_rate * mbuf[here] + sbuf[here]

    for k, (c, d) in enumerate(order):
        momentum(c, d)
        if k == 0:
            pl.semaphore_wait(barrier, nf + nt - 2)
        else:
            send(*order[k - 1])
    send(*order[-1])

    for c in range(chunks + 1):
        if c < chunks:
            grams(c)
        if c > 0:
            apply(c - 1)
        if c < chunks:
            factors(c)

    fetch.wait()
    for c in range(chunks):
        for d in range(nf):
            if d > 0:
                back(c, d).wait_recv()
            else:
                keep(c).wait()
            here = pl.ds(lax.rem(me_f - d + nf, nf) * share + c * per, per)
            new[here] = wbuf[here] - learn_rate * out[here]

    for c in range(chunks):
        for d in range(1, nf):
            there(c, d).wait_send()
            back(c, d).wait_send()
        for d in range(1, nt):
            gram_copy(c, d).wait_send()
            factor_copy(c, d).wait_send()


def finish(new, mom, new_out, mom_out, sems):
    copies = []
    for k, (src, dst) in enumerate(((mom, mom_out), (new, new_out))):
        copies.append(pltpu.make_async_copy(src, dst, sems.at[k]))
    for copy in copies:
        copy.start()
    for copy in copies:
        copy.wait()


def stepped(nf, nt, slopes_in, moments_in, weights_in):
    mats, rows, wide = slopes_in.shape
    side, share = rows * nf, mats // nf
    most = share // nt
    chunks = max(k for k in range(1, 5) if most % k == 0)
    per = share // chunks
    each = per // nt
    vmem, dma = pltpu.VMEM, pltpu.SemaphoreType.DMA
    shape = jax.ShapeDtypeStruct(slopes_in.shape, jnp.float32)
    held = [pl.BlockSpec(memory_space=pltpu.VMEM)] * 2
    far = [pl.BlockSpec(memory_space=pltpu.HBM)]
    results = pl.pallas_call(
        functools.partial(kernel, nf, nt, chunks),
        out_shape=[shape] * 2,
        in_specs=far * 3,
        out_specs=held,
        scratch_shapes=[
            vmem(slopes_in.shape, jnp.float32),
            vmem(slopes_in.shape, jnp.float32),
            vmem(slopes_in.shape, jnp.float32),
            vmem(slopes_in.shape, jnp.float32),
            vmem((share, side, wide), jnp.float32),
            vmem((chunks, nt - 1, each, side, side), jnp.float32),
            vmem((chunks, nt, each, side, side), jnp.float32),
            vmem((chunks, nt, each, side, side), jnp.float32),
            vmem((share, side, wide), jnp.float32),
            dma((chunks, nf - 1)), dma((chunks, nf - 1)),
            dma((chunks, nt - 1)), dma((chunks, nt - 1)),
            dma((chunks, nt - 1)), dma((chunks, nt - 1)),
            dma((chunks, nf - 1)), dma((chunks, nf - 1)),
            dma((3, chunks)), dma((2, chunks, nf)),
        ],
        compiler_params=pltpu.CompilerParams(
            collective_id=0, has_side_effects=True, vmem_limit_bytes=32 * 2**20
        ),
    )(*(pltpu.with_memory_space_constraint(x, pltpu.HBM) for x in (slopes_in, moments_in, weights_in)))
    return pl.pallas_call(
        finish,
        out_shape=[shape] * 2,
        in_specs=held,
        out_specs=far * 2,
        scratch_shapes=[dma((2,))],
        compiler_params=pltpu.CompilerParams(vmem_limit_bytes=2**20),
    )(*results)


def orthogonal_plain(new_momentum):
    moved = lax.all_to_all(new_momentum, "fsdp", split_axis=0, concat_axis=1, tiled=True)
    gram = lax.dot_general(moved, moved, (((2,), (2,)), ((0,), (0,))), precision=HIGHEST)
    gram = lax.psum_scatter(gram, "tp", scatter_dimension=0, tiled=True)
    factors = lax.all_gather(jax.vmap(factor_of)(gram), "tp", axis=0, tiled=True)
    whole = lax.dot_general(factors, moved, (((2,), (1,)), ((0,), (0,))), precision=HIGHEST)
    return lax.all_to_all(whole, "fsdp", split_axis=1, concat_axis=0, tiled=True)


def body(nf, nt, slopes_in, moments_in, weights_in):
    rows, wide = slopes_in.shape[1:]
    if rows % 8 == 0 and wide % 128 == 0:
        return stepped(nf, nt, slopes_in, moments_in, weights_in)
    new_momentum = hold_rate * moments_in + slopes_in
    new_weights = weights_in - learn_rate * orthogonal_plain(new_momentum)
    return (new_weights, new_momentum)


def solution(mesh):
    placed = (P("job", "fsdp", "tp"), P("job", "fsdp", "tp"), P("job", "fsdp", "tp"))
    return jax.shard_map(
        functools.partial(body, mesh.shape["fsdp"], mesh.shape["tp"]),
        mesh=mesh,
        in_specs=placed,
        out_specs=(P("job", "fsdp", "tp"), P("job", "fsdp", "tp")),
        check_vma=False,
    )
```

profile of v0, /device:TPU:0, one launch (start us, length us, event | category | flops | bytes accessed | tf_op | source)
XLA Modules:
  0.0 99.2 jit_solution(1462658984015305055)
XLA Ops:
  0.6 96.5 %shard_map.50 = (f32[64,32,256]{2,1,0:T(8,128)S(1)}, f32[64,32,256]{2,1,0:T(8,128)S(1)}) custom-call(f32[64,32,256]{2,1,0:T(8,128)} %slopes.1, f32[64,32,256]{2,1,0:T(8,128)} %moments.1, f32[64,32,256]{2,1,0:T(8,128)} %weights.1), custom_call_target="tpu_custom_call" | custom-call | tf_op jit(solution)/shard_map/pallas_call | solution.py:233
  97.2 2.0 %shard_map.51 = (f32[64,32,256]{2,1,0:T(8,128)}, f32[64,32,256]{2,1,0:T(8,128)}) custom-call(f32[64,32,256]{2,1,0:T(8,128)S(1)} %get-tuple-element.4.new, f32[64,32,256]{2,1,0:T(8,128)S(1)} %get-tuple-element.5.mom), custom_call_target="tpu_custom_call" | custom-call | tf_op jit(solution)/shard_map/pallas_call | solution.py:258
where the time goes:
time: 99.4 us; the launch traced here: 99.2 us
  Pallas kernels  98.6 us (99%)
    pallas_call x1, Pallas kernels, stepped(): pl.pallas_call(functools.partial(kernel, nf, nt, chunks), out_shape=[shap...  96.5 us
    pallas_call x1, Pallas kernels, stepped(): pl.pallas_call(finish, out_shape=[shape] * 2, in_specs=held, out_specs=fa...  2.03 us

commit v1 on v0

v1 whole, which is shorter than its diff:
```python
import functools

import jax
import jax.numpy as jnp
from jax import lax
from jax.experimental import pallas as pl
from jax.experimental.pallas import tpu as pltpu
from jax.sharding import PartitionSpec as P

ITERS = 5
LINE = 4


hold_rate = 0.9
learn_rate = 0.8

COEF_A, COEF_B, COEF_C = 3.4445, -4.775, 2.0315
MESH = pl.DeviceIdType.MESH
HIGHEST = lax.Precision.HIGHEST


def dot(a, b, contract=((1,), (0,))):
    return lax.dot_general(
        a, b, (contract, ((), ())), precision=HIGHEST, preferred_element_type=jnp.float32
    )


def factor_of(gram):
    side = gram.shape[0]
    rows = lax.broadcasted_iota(jnp.int32, (side, side), 0)
    eye = rows == lax.broadcasted_iota(jnp.int32, (side, side), 1)
    total = jnp.sum(jnp.where(eye, gram, 0.0), axis=(0, 1), keepdims=True)
    scale = lax.rsqrt(total + 1e-06)

    def mixed_of(a):
        return COEF_B * a + COEF_C * dot(a, a)

    def step(_, carry):
        a, q = carry
        mixed = mixed_of(a)
        half = COEF_A * a + dot(mixed, a)
        return COEF_A * half + dot(half, mixed), COEF_A * q + dot(mixed, q)

    a = gram * scale * scale
    q = jnp.where(eye, jnp.broadcast_to(scale, gram.shape), 0.0)
    a, q = lax.fori_loop(0, ITERS - 1, step, (a, q))
    return COEF_A * q + dot(mixed_of(a), q)


def kernel(nt, chunks, slopes, moments, weights, new, mom, out, wbuf, sbuf, mbuf, xbuf, gsend, grecv, qrecv, ybuf, sends, frecv, gr, qr, brecv, loads, hello, ready):
    me_f, me_t = lax.axis_index("fsdp"), lax.axis_index("tp")
    mats, rows, _ = mom.shape
    share = mats // LINE
    per = share // chunks
    each = per // nt

    half = me_f // 2
    far, near, side = 3 - 3 * half, 2 - half, me_f + 1 - 2 * lax.rem(me_f, 2)
    inner = me_f * (3 - me_f) > 0
    outer = me_f * (3 - me_f) == 0
    barrier = pltpu.get_barrier_semaphore()

    def tell(semaphore, device):
        pl.semaphore_signal(semaphore, inc=1, device_id=device, device_id_type=MESH)

    def tell_tp(semaphore):
        for d in range(1, nt):
            tell(semaphore, {"tp": lax.rem(me_t + d, nt)})

    @pl.when(inner)
    def _():
        tell(barrier, {"fsdp": near})

    @pl.when(outer)
    def _():
        tell_tp(barrier)

    order = [(c, peer) for c in range(chunks) for peer in (near, far, side, me_f)]

    def block(c, peer):
        return pl.ds(peer * share + c * per, per)

    def count(k):
        return k if k < 4 else 3 + k // 4

    def load(k):
        here = block(*order[k])
        return (
            pltpu.make_async_copy(slopes.at[here], sbuf.at[here], loads.at[count(k)]),
            pltpu.make_async_copy(moments.at[here], mbuf.at[here], loads.at[count(k)]),
        )

    for k in range(len(order)):
        for copy in load(k):
            copy.start()
    fetch = pltpu.make_async_copy(weights, wbuf, loads.at[count(len(order))])
    fetch.start()

    def loaded(k):
        if k < 4:
            some = pl.ds(0, 2 * per)
        elif k % 4 == 0:
            some = pl.ds(0, 8 * per)
        else:
            return
        pltpu.make_async_copy(slopes.at[some], sbuf.at[some], loads.at[count(k)]).wait()

    my_rows = pl.ds(pl.multiple_of(me_f * rows, rows), rows)

    def there(c, peer):
        return pltpu.make_async_remote_copy(
            src_ref=mom.at[block(c, peer)],
            dst_ref=xbuf.at[pl.ds(c * per, per), my_rows, :],
            send_sem=sends.at[0], recv_sem=frecv.at[c],
            device_id={"fsdp": peer}, device_id_type=MESH,
        )

    def back(c, peer):
        theirs = pl.ds(pl.multiple_of(peer * rows, rows), rows)
        return pltpu.make_async_remote_copy(
            src_ref=ybuf.at[pl.ds(c * per, per), theirs, :],
            dst_ref=out.at[block(c, me_f)],
            send_sem=sends.at[1], recv_sem=brecv.at[c],
            device_id={"fsdp": peer}, device_id_type=MESH,
        )

    def gram_copy(c, d):
        return pltpu.make_async_remote_copy(
            src_ref=gsend.at[c, d - 1], dst_ref=grecv.at[c, d],
            send_sem=sends.at[2], recv_sem=gr.at[c],
            device_id={"tp": lax.rem(me_t + d, nt)}, device_id_type=MESH,
        )

    def factor_copy(c, d):
        return pltpu.make_async_remote_copy(
            src_ref=qrecv.at[c, 0], dst_ref=qrecv.at[c, d],
            send_sem=sends.at[3], recv_sem=qr.at[c],
            device_id={"tp": lax.rem(me_t + d, nt)}, device_id_type=MESH,
        )

    def landed(ref, semaphore):
        pltpu.make_async_copy(ref, ref, semaphore).wait()

    def rows_landed(c, semaphores):
        landed(out.at[pl.ds(0, (LINE - 1) * per)], semaphores.at[c])

    def grams(c):
        rows_landed(c, frecv)
        for d in list(range(1, nt)) + [0]:
            first = c * per + lax.rem(me_t + d, nt) * each
            for e in range(each):
                x = xbuf[first + e]
                g = dot(x, x, ((1,), (1,)))
                if d == 0:
                    grecv[c, 0, e] = g
                else:
                    gsend[c, d - 1, e] = g
            if d > 0:
                gram_copy(c, d).start()

    def factors(c):
        landed(gsend.at[0], gr.at[c])
        for e in range(each):
            g = grecv[c, 0, e]
            for d in range(1, nt):
                g = g + grecv[c, d, e]
            qrecv[c, 0, e] = factor_of(g)
        for d in range(1, nt):
            factor_copy(c, d).start()

    def apply(c):
        for d in range(nt):
            if d == 1:
                landed(gsend.at[0], qr.at[c])
            first = c * per + lax.rem(me_t - d + nt, nt) * each
            for e in range(each):
                ybuf[first + e] = dot(qrecv[c, d, e], xbuf[first + e])
        for peer in (far, near, side):
            back(c, peer).start()
        out[block(c, me_f)] = ybuf[pl.ds(c * per, per), my_rows, :]

    def momentum(k):
        loaded(k)
        c, peer = order[k]
        here = block(c, peer)
        value = hold_rate * mbuf[here] + sbuf[here]
        mom[here] = value
        if k % 4 == 3:
            xbuf[pl.ds(c * per, per), my_rows, :] = value

    momentum(0)
    momentum(1)

    @pl.when(inner)
    def _():
        pl.semaphore_wait(barrier, 1)
        there(0, near).start()
        tell(barrier, {"fsdp": side})

    for k in range(2, len(order)):
        momentum(k)

    @pl.when(inner)
    def _():
        for c in range(1, min(chunks, 2)):
            there(c, near).start()
        pl.semaphore_wait(hello, 2)
        tell(hello, {"fsdp": side})
        for c in range(chunks):
            for peer in (near, far, side) if c > 1 else (far, side):
                there(c, peer).start()
        pl.semaphore_wait(ready, 1)

    @pl.when(outer)
    def _():
        pl.semaphore_wait(barrier, nt)
        tell(hello, {"fsdp": side})
        tell(hello, {"fsdp": near})
        for c in range(min(chunks, 2)):
            for peer in (near, side):
                there(c, peer).start()
        pl.semaphore_wait(hello, 1)
        for c in range(chunks):
            for peer in (near, far, side) if c > 1 else (far,):
                there(c, peer).start()
        tell_tp(ready)
        pl.semaphore_wait(ready, nt - 1)
        tell(ready, {"fsdp": side})

    grams(0)
    factors(0)
    apply(0)
    for c in range(1, chunks + 1):
        if c < chunks:
            grams(c)
        if c > 1:
            apply(c - 1)
        if c < chunks:
            factors(c)

    fetch.wait()
    for c in range(chunks):
        rows_landed(c, brecv)
        for peer in range(LINE):
            here = pl.ds(peer * share + c * per, per)
            new[here] = wbuf[here] - learn_rate * out[here]

    landed(mom.at[pl.ds(0, mats - share)], sends.at[0])
    landed(mom.at[pl.ds(0, mats - share)], sends.at[1])
    landed(gsend, sends.at[2])
    landed(gsend, sends.at[3])


def finish(new, mom, new_out, mom_out, sems):
    copies = []
    for k, (src, dst) in enumerate(((mom, mom_out), (new, new_out))):
        copies.append(pltpu.make_async_copy(src, dst, sems.at[k]))
    for copy in copies:
        copy.start()
    for copy in copies:
        copy.wait()


def stepped(nf, nt, slopes_in, moments_in, weights_in):
    mats, rows, wide = slopes_in.shape
    side, share = rows * nf, mats // nf
    most = share // nt
    chunks = max(k for k in range(1, 5) if most % k == 0)
    per = share // chunks
    each = per // nt
    vmem, dma, flag = pltpu.VMEM, pltpu.SemaphoreType.DMA, pltpu.SemaphoreType.REGULAR
    shape = jax.ShapeDtypeStruct(slopes_in.shape, jnp.float32)
    held = [pl.BlockSpec(memory_space=pltpu.VMEM)] * 2
    far = [pl.BlockSpec(memory_space=pltpu.HBM)]
    results = pl.pallas_call(
        functools.partial(kernel, nt, chunks),
        out_shape=[shape] * 2,
        in_specs=far * 3,
        out_specs=held,
        scratch_shapes=[
            vmem(slopes_in.shape, jnp.float32),
            vmem(slopes_in.shape, jnp.float32),
            vmem(slopes_in.shape, jnp.float32),
            vmem(slopes_in.shape, jnp.float32),
            vmem((share, side, wide), jnp.float32),
            vmem((chunks, nt - 1, each, side, side), jnp.float32),
            vmem((chunks, nt, each, side, side), jnp.float32),
            vmem((chunks, nt, each, side, side), jnp.float32),
            vmem((share, side, wide), jnp.float32),
            dma((4,)), dma((chunks,)), dma((chunks,)), dma((chunks,)), dma((chunks,)),
            dma((4 + chunks,)), flag, flag,
        ],
        compiler_params=pltpu.CompilerParams(
            collective_id=0, has_side_effects=True, vmem_limit_bytes=32 * 2**20
        ),
    )(*(pltpu.with_memory_space_constraint(x, pltpu.HBM) for x in (slopes_in, moments_in, weights_in)))
    return pl.pallas_call(
        finish,
        out_shape=[shape] * 2,
        in_specs=held,
        out_specs=far * 2,
        scratch_shapes=[dma((2,))],
        compiler_params=pltpu.CompilerParams(vmem_limit_bytes=2**20),
    )(*results)


def orthogonal_plain(new_momentum):
    moved = lax.all_to_all(new_momentum, "fsdp", split_axis=0, concat_axis=1, tiled=True)
    gram = lax.dot_general(moved, moved, (((2,), (2,)), ((0,), (0,))), precision=HIGHEST)
    gram = lax.psum_scatter(gram, "tp", scatter_dimension=0, tiled=True)
    factors = lax.all_gather(jax.vmap(factor_of)(gram), "tp", axis=0, tiled=True)
    whole = lax.dot_general(factors, moved, (((2,), (1,)), ((0,), (0,))), precision=HIGHEST)
    return lax.all_to_all(whole, "fsdp", split_axis=1, concat_axis=0, tiled=True)


def body(nf, nt, slopes_in, moments_in, weights_in):
    rows, wide = slopes_in.shape[1:]
    if nf == LINE and nt > 1 and rows % 8 == 0 and wide % 128 == 0:
        return stepped(nf, nt, slopes_in, moments_in, weights_in)
    new_momentum = hold_rate * moments_in + slopes_in
    new_weights = weights_in - learn_rate * orthogonal_plain(new_momentum)
    return (new_weights, new_momentum)


def solution(mesh):
    placed = (P("job", "fsdp", "tp"), P("job", "fsdp", "tp"), P("job", "fsdp", "tp"))
    return jax.shard_map(
        functools.partial(body, mesh.shape["fsdp"], mesh.shape["tp"]),
        mesh=mesh,
        in_specs=placed,
        out_specs=(P("job", "fsdp", "tp"), P("job", "fsdp", "tp")),
        check_vma=False,
    )
```

time: 99.4 us -> 97.2 us (0.978)
  the two profiles are of different devices: /device:TPU:0 before, /device:TPU:15 now
where the time goes in v1:
time: 97.2 us; the launch traced here: 95.9 us
  Pallas kernels  95.3 us (98%)
    pallas_call x1, Pallas kernels, stepped(): pl.pallas_call(functools.partial(kernel, nt, chunks), out_shape=[shape] *...  93.2 us
    pallas_call x1, Pallas kernels, stepped(): pl.pallas_call(finish, out_shape=[shape] * 2, in_specs=held, out_specs=fa...  2.03 us

profile of v1, /device:TPU:15, one launch (start us, length us, event | category | flops | bytes accessed | tf_op | source)
XLA Modules:
  0.0 95.9 jit_solution(12435184852845391089)
XLA Ops:
  0.6 93.2 %shard_map.50 = (f32[64,32,256]{2,1,0:T(8,128)S(1)}, f32[64,32,256]{2,1,0:T(8,128)S(1)}) custom-call(f32[64,32,256]{2,1,0:T(8,128)} %slopes.1, f32[64,32,256]{2,1,0:T(8,128)} %moments.1, f32[64,32,256]{2,1,0:T(8,128)} %weights.1), custom_call_target="tpu_custom_call" | custom-call | tf_op jit(solution)/shard_map/pallas_call | solution.py:275
  93.9 2.0 %shard_map.51 = (f32[64,32,256]{2,1,0:T(8,128)}, f32[64,32,256]{2,1,0:T(8,128)}) custom-call(f32[64,32,256]{2,1,0:T(8,128)S(1)} %get-tuple-element.4.new, f32[64,32,256]{2,1,0:T(8,128)S(1)} %get-tuple-element.5.mom), custom_call_target="tpu_custom_call" | custom-call | tf_op jit(solution)/shard_map/pallas_call | solution.py:297

commit v2 on v1

--- a/solution.py
+++ b/solution.py
@@ -9,6 +9,7 @@
 
 ITERS = 5
 LINE = 4
+AHEAD = 2
 
 
 hold_rate = 0.9
@@ -47,7 +48,7 @@
     return COEF_A * q + dot(mixed_of(a), q)
 
 
-def kernel(nt, chunks, slopes, moments, weights, new, mom, out, wbuf, sbuf, mbuf, xbuf, gsend, grecv, qrecv, ybuf, sends, frecv, gr, qr, brecv, loads, hello, ready):
+def kernel(nt, chunks, slopes, moments, weights, early, new, mom, out, wbuf, inputs, xbuf, gsend, grecv, qrecv, ybuf, sends, frecv, gr, qr, brecv, loads, hello, ready):
     me_f, me_t = lax.axis_index("fsdp"), lax.axis_index("tp")
     mats, rows, _ = mom.shape
     share = mats // LINE
@@ -80,30 +81,19 @@
     def block(c, peer):
         return pl.ds(peer * share + c * per, per)
 
-    def count(k):
-        return k if k < 4 else 3 + k // 4
-
-    def load(k):
-        here = block(*order[k])
-        return (
-            pltpu.make_async_copy(slopes.at[here], sbuf.at[here], loads.at[count(k)]),
-            pltpu.make_async_copy(moments.at[here], mbuf.at[here], loads.at[count(k)]),
-        )
-
-    for k in range(len(order)):
-        for copy in load(k):
-            copy.start()
-    fetch = pltpu.make_async_copy(weights, wbuf, loads.at[count(len(order))])
-    fetch.start()
-
-    def loaded(k):
-        if k < 4:
-            some = pl.ds(0, 2 * per)
-        elif k % 4 == 0:
-            some = pl.ds(0, 8 * per)
-        else:
-            return
-        pltpu.make_async_copy(slopes.at[some], sbuf.at[some], loads.at[count(k)]).wait()
+    groups = [(0, 1), (1, LINE), (LINE, 2 * LINE), (2 * LINE, chunks * LINE)]
+
+    def request(group):
+        for k in range(*groups[group]):
+            here = block(*order[k])
+            pltpu.make_async_copy(slopes.at[here], inputs.at[0, here], loads.at[group]).start()
+            pltpu.make_async_copy(moments.at[here], inputs.at[1, here], loads.at[group]).start()
+
+    def landed(ref, semaphore):
+        pltpu.make_async_copy(ref, ref, semaphore).wait()
+
+    request(0)
+    fetch = pltpu.make_async_copy(weights, wbuf, loads.at[len(groups)])
 
     my_rows = pl.ds(pl.multiple_of(me_f * rows, rows), rows)
 
@@ -137,9 +127,6 @@
             send_sem=sends.at[3], recv_sem=qr.at[c],
             device_id={"tp": lax.rem(me_t + d, nt)}, device_id_type=MESH,
         )
-
-    def landed(ref, semaphore):
-        pltpu.make_async_copy(ref, ref, semaphore).wait()
 
     def rows_landed(c, semaphores):
         landed(out.at[pl.ds(0, (LINE - 1) * per)], semaphores.at[c])
@@ -179,17 +166,20 @@
             back(c, peer).start()
         out[block(c, me_f)] = ybuf[pl.ds(c * per, per), my_rows, :]
 
-    def momentum(k):
-        loaded(k)
-        c, peer = order[k]
-        here = block(c, peer)
-        value = hold_rate * mbuf[here] + sbuf[here]
-        mom[here] = value
-        if k % 4 == 3:
-            xbuf[pl.ds(c * per, per), my_rows, :] = value
+    def momentum(group):
+        first, last = groups[group]
+        if last > first:
+            landed(inputs.at[:, pl.ds(0, (last - first) * per)], loads.at[group])
+        for k in range(first, last):
+            c, peer = order[k]
+            here = block(c, peer)
+            value = hold_rate * inputs[1, here] + inputs[0, here]
+            mom[here] = value
+            if k % LINE == LINE - 1:
+                xbuf[pl.ds(c * per, per), my_rows, :] = value
 
     momentum(0)
-    momentum(1)
+    request(1)
 
     @pl.when(inner)
     def _():
@@ -197,17 +187,20 @@
         there(0, near).start()
         tell(barrier, {"fsdp": side})
 
-    for k in range(2, len(order)):
-        momentum(k)
+    request(2)
+    request(3)
+    fetch.start()
+    for group in range(1, len(groups)):
+        momentum(group)
 
     @pl.when(inner)
     def _():
-        for c in range(1, min(chunks, 2)):
+        for c in range(1, min(chunks, AHEAD)):
             there(c, near).start()
         pl.semaphore_wait(hello, 2)
         tell(hello, {"fsdp": side})
         for c in range(chunks):
-            for peer in (near, far, side) if c > 1 else (far, side):
+            for peer in (near, far, side) if c >= AHEAD else (far, side):
                 there(c, peer).start()
         pl.semaphore_wait(ready, 1)
 
@@ -216,12 +209,12 @@
         pl.semaphore_wait(barrier, nt)
         tell(hello, {"fsdp": side})
         tell(hello, {"fsdp": near})
-        for c in range(min(chunks, 2)):
+        for c in range(min(chunks, AHEAD)):
             for peer in (near, side):
                 there(c, peer).start()
         pl.semaphore_wait(hello, 1)
         for c in range(chunks):
-            for peer in (near, far, side) if c > 1 else (far,):
+            for peer in (near, far, side) if c >= AHEAD else (far,):
                 there(c, peer).start()
         tell_tp(ready)
         pl.semaphore_wait(ready, nt - 1)
@@ -251,14 +244,34 @@
     landed(gsend, sends.at[3])
 
 
-def finish(new, mom, new_out, mom_out, sems):
-    copies = []
-    for k, (src, dst) in enumerate(((mom, mom_out), (new, new_out))):
-        copies.append(pltpu.make_async_copy(src, dst, sems.at[k]))
-    for copy in copies:
-        copy.start()
-    for copy in copies:
-        copy.wait()
+def early_momentum(slopes, moments, mom_out, inputs, held, loads, writes):
+    @pl.when(lax.axis_index("fsdp") == 0)
+    def _():
+        parts = loads.shape[0]
+        some = mom_out.shape[0] // parts
+
+        def part(j):
+            return pl.ds(j * some, some)
+
+        for j in range(parts):
+            pltpu.make_async_copy(slopes.at[part(j)], inputs.at[0, part(j)], loads.at[j]).start()
+            pltpu.make_async_copy(moments.at[part(j)], inputs.at[1, part(j)], loads.at[j]).start()
+        for j in range(parts):
+            arrived = inputs.at[:, part(j)]
+            pltpu.make_async_copy(arrived, arrived, loads.at[j]).wait()
+            held[part(j)] = hold_rate * inputs[1, part(j)] + inputs[0, part(j)]
+            pltpu.make_async_copy(held.at[part(j)], mom_out.at[part(j)], writes).start()
+        pltpu.make_async_copy(held, mom_out, writes).wait()
+
+
+def finish(new, mom, early, new_out, mom_out, sems):
+    late = lax.axis_index("fsdp") > 0
+    rest = pltpu.make_async_copy(mom, mom_out, sems.at[0])
+    pl.when(late)(rest.start)
+    last = pltpu.make_async_copy(new, new_out, sems.at[1])
+    last.start()
+    pl.when(late)(rest.wait)
+    last.wait()
 
 
 def stepped(nf, nt, slopes_in, moments_in, weights_in):
@@ -272,36 +285,50 @@
     shape = jax.ShapeDtypeStruct(slopes_in.shape, jnp.float32)
     held = [pl.BlockSpec(memory_space=pltpu.VMEM)] * 2
     far = [pl.BlockSpec(memory_space=pltpu.HBM)]
-    results = pl.pallas_call(
+    inputs = [pltpu.with_memory_space_constraint(x, pltpu.HBM) for x in (slopes_in, moments_in, weights_in)]
+    early = pl.pallas_call(
+        early_momentum,
+        out_shape=shape,
+        in_specs=far * 2,
+        out_specs=far[0],
+        scratch_shapes=[
+            vmem((2,) + slopes_in.shape, jnp.float32),
+            vmem(slopes_in.shape, jnp.float32),
+            dma((max(k for k in range(1, 5) if mats % k == 0),)), dma,
+        ],
+        compiler_params=pltpu.CompilerParams(vmem_limit_bytes=16 * 2**20),
+    )(*inputs[:2])
+    early = pltpu.with_memory_space_constraint(early, pltpu.HBM)
+    new, mom = pl.pallas_call(
         functools.partial(kernel, nt, chunks),
         out_shape=[shape] * 2,
-        in_specs=far * 3,
+        in_specs=far * 4,
         out_specs=held,
         scratch_shapes=[
             vmem(slopes_in.shape, jnp.float32),
             vmem(slopes_in.shape, jnp.float32),
-            vmem(slopes_in.shape, jnp.float32),
-            vmem(slopes_in.shape, jnp.float32),
+            vmem((2,) + slopes_in.shape, jnp.float32),
             vmem((share, side, wide), jnp.float32),
             vmem((chunks, nt - 1, each, side, side), jnp.float32),
             vmem((chunks, nt, each, side, side), jnp.float32),
             vmem((chunks, nt, each, side, side), jnp.float32),
             vmem((share, side, wide), jnp.float32),
             dma((4,)), dma((chunks,)), dma((chunks,)), dma((chunks,)), dma((chunks,)),
-            dma((4 + chunks,)), flag, flag,
+            dma((5,)), flag, flag,
         ],
         compiler_params=pltpu.CompilerParams(
             collective_id=0, has_side_effects=True, vmem_limit_bytes=32 * 2**20
         ),
-    )(*(pltpu.with_memory_space_constraint(x, pltpu.HBM) for x in (slopes_in, moments_in, weights_in)))
+    )(*inputs, early)
     return pl.pallas_call(
         finish,
         out_shape=[shape] * 2,
-        in_specs=held,
+        in_specs=held + far,
         out_specs=far * 2,
+        input_output_aliases={2: 1},
         scratch_shapes=[dma((2,))],
         compiler_params=pltpu.CompilerParams(vmem_limit_bytes=2**20),
-    )(*results)
+    )(new, mom, early)
 
 
 def orthogonal_plain(new_momentum):

time: 97.2 us -> 96.6 us (level)
    pallas_call x1 -> x2, Pallas kernels: 2.03 us -> 2.1 us  [the longest x1 2.04 us: stepped(): pl.pallas_call(finish, out_shape=[shape] * 2, in_specs=held + far, out_sp...]
where the time goes in v2:
time: 96.6 us; the launch traced here: 96.1 us
  Pallas kernels  95.5 us (99%)
    pallas_call x1, Pallas kernels, stepped(): pl.pallas_call(functools.partial(kernel, nt, chunks), out_shape=[shape] *...  93.4 us
    pallas_call x1, Pallas kernels, stepped(): pl.pallas_call(finish, out_shape=[shape] * 2, in_specs=held + far, out_sp...  2.04 us

profile of v2, /device:TPU:15, one launch (start us, length us, event | category | flops | bytes accessed | tf_op | source)
XLA Modules:
  0.0 96.1 jit_solution(4626110091087925121)
XLA Ops:
  0.6 0.1 shard_map.50.early
  0.7 93.4 %shard_map.51 = (f32[64,32,256]{2,1,0:T(8,128)S(1)}, f32[64,32,256]{2,1,0:T(8,128)S(1)}) custom-call(f32[64,32,256]{2,1,0:T(8,128)} %slopes.3, f32[64,32,256]{2,1,0:T(8,128)} %moments.3, f32[64,32,256]{2,1,0:T(8,128)} %weights.1, f32[64,32,256]{2,1,0:T(8,128)} %shard_map.50.early), custom_call_target="tpu_custom_call" | custom-call | tf_op jit(solution)/shard_map/pallas_call | solution.py:302
  94.1 2.0 %shard_map.52 = (f32[64,32,256]{2,1,0:T(8,128)}, f32[64,32,256]{2,1,0:T(8,128)}) custom-call(f32[64,32,256]{2,1,0:T(8,128)S(1)} %get-tuple-element.4.new, f32[64,32,256]{2,1,0:T(8,128)S(1)} %get-tuple-element.5.mom, f32[64,32,256]{2,1,0:T(8,128)} %shard_map.50.early), custom_call_target="tpu_custom_call", output_to_operand_aliasing={{1}: (2, {})} | custom-call | tf_op jit(solution)/shard_map/pallas_call | solution.py:323

commit v3 on v2

--- a/solution.py
+++ b/solution.py
@@ -10,6 +10,9 @@
 ITERS = 5
 LINE = 4
 AHEAD = 2
+LATE_CHUNKS = (1, 2)
+CHUNKS = 4
+ORDER = ((0, 0), (1, 0), (2, 0), (0, 1), (1, 1), (0, 2), (2, 1), (1, 2), (0, 3), (1, 3), (2, 2), (2, 3))
 
 
 hold_rate = 0.9
@@ -48,21 +51,75 @@
     return COEF_A * q + dot(mixed_of(a), q)
 
 
-def kernel(nt, chunks, slopes, moments, weights, early, new, mom, out, wbuf, inputs, xbuf, gsend, grecv, qrecv, ybuf, sends, frecv, gr, qr, brecv, loads, hello, ready):
-    me_f, me_t = lax.axis_index("fsdp"), lax.axis_index("tp")
+def places():
+    me_f = lax.axis_index("fsdp")
+    half = me_f // 2
+    return me_f, 3 - 3 * half, 2 - half, me_f + 1 - 2 * lax.rem(me_f, 2)
+
+
+def tell(semaphore, device):
+    pl.semaphore_signal(semaphore, inc=1, device_id=device, device_id_type=MESH)
+
+
+def landed(ref, semaphore):
+    pltpu.make_async_copy(ref, ref, semaphore).wait()
+
+
+def pieces_of(share, chunks):
+    per = share // chunks
+    return [(c * per, per) for c in range(chunks)]
+
+
+def each_job(pieces, act):
+    kind = lax.rem(lax.axis_index("job"), 2)
+    for number, late in enumerate(LATE_CHUNKS):
+        pl.when(kind == number)(functools.partial(act, len(pieces) - late))
+
+
+def back_copy(ybuf, out, sends, arrivals, share, me_f, peer, piece):
+    start, size = piece
+    rows = out.shape[1]
+    theirs = pl.ds(pl.multiple_of(peer * rows, rows), rows)
+    return pltpu.make_async_remote_copy(
+        src_ref=ybuf.at[pl.ds(start, size), theirs, :],
+        dst_ref=out.at[pl.ds(me_f * share + start, size)],
+        send_sem=sends, recv_sem=arrivals,
+        device_id={"fsdp": peer}, device_id_type=MESH,
+    )
+
+
+def own_rows(ybuf, out, share, me_f, piece):
+    start, size = piece
+    rows = out.shape[1]
+    mine = pl.ds(pl.multiple_of(me_f * rows, rows), rows)
+    out[pl.ds(me_f * share + start, size)] = ybuf[pl.ds(start, size), mine, :]
+
+
+def update(new, wbuf, out, arrivals, share, piece):
+    start, size = piece
+    landed(out.at[pl.ds(0, (LINE - 1) * size)], arrivals)
+    for owner in range(LINE):
+        here = pl.ds(owner * share + start, size)
+        new[here] = wbuf[here] - learn_rate * out[here]
+
+
+def sent(out, sends, pieces):
+    total = sum(size for _, size in pieces)
+    landed(out.at[pl.ds(0, (LINE - 1) * total)], sends)
+
+
+def kernel(nt, chunks, slopes, moments, weights, new, mom, ybuf, wbuf, out, inputs, xbuf, gsend, grecv, qrecv, sends, frecv, gr, qr, brecv, loads, hello, ready):
+    me_f, far, near, side = places()
+    me_t = lax.axis_index("tp")
     mats, rows, _ = mom.shape
     share = mats // LINE
     per = share // chunks
     each = per // nt
-
-    half = me_f // 2
-    far, near, side = 3 - 3 * half, 2 - half, me_f + 1 - 2 * lax.rem(me_f, 2)
+    pieces = pieces_of(share, chunks)
+
     inner = me_f * (3 - me_f) > 0
     outer = me_f * (3 - me_f) == 0
     barrier = pltpu.get_barrier_semaphore()
-
-    def tell(semaphore, device):
-        pl.semaphore_signal(semaphore, inc=1, device_id=device, device_id_type=MESH)
 
     def tell_tp(semaphore):
         for d in range(1, nt):
@@ -88,9 +145,6 @@
             here = block(*order[k])
             pltpu.make_async_copy(slopes.at[here], inputs.at[0, here], loads.at[group]).start()
             pltpu.make_async_copy(moments.at[here], inputs.at[1, here], loads.at[group]).start()
-
-    def landed(ref, semaphore):
-        pltpu.make_async_copy(ref, ref, semaphore).wait()
 
     request(0)
     fetch = pltpu.make_async_copy(weights, wbuf, loads.at[len(groups)])
@@ -105,15 +159,6 @@
             device_id={"fsdp": peer}, device_id_type=MESH,
         )
 
-    def back(c, peer):
-        theirs = pl.ds(pl.multiple_of(peer * rows, rows), rows)
-        return pltpu.make_async_remote_copy(
-            src_ref=ybuf.at[pl.ds(c * per, per), theirs, :],
-            dst_ref=out.at[block(c, me_f)],
-            send_sem=sends.at[1], recv_sem=brecv.at[c],
-            device_id={"fsdp": peer}, device_id_type=MESH,
-        )
-
     def gram_copy(c, d):
         return pltpu.make_async_remote_copy(
             src_ref=gsend.at[c, d - 1], dst_ref=grecv.at[c, d],
@@ -128,11 +173,8 @@
             device_id={"tp": lax.rem(me_t + d, nt)}, device_id_type=MESH,
         )
 
-    def rows_landed(c, semaphores):
-        landed(out.at[pl.ds(0, (LINE - 1) * per)], semaphores.at[c])
-
     def grams(c):
-        rows_landed(c, frecv)
+        landed(out.at[pl.ds(0, (LINE - 1) * per)], frecv.at[c])
         for d in list(range(1, nt)) + [0]:
             first = c * per + lax.rem(me_t + d, nt) * each
             for e in range(each):
@@ -162,9 +204,15 @@
             first = c * per + lax.rem(me_t - d + nt, nt) * each
             for e in range(each):
                 ybuf[first + e] = dot(qrecv[c, d, e], xbuf[first + e])
-        for peer in (far, near, side):
-            back(c, peer).start()
-        out[block(c, me_f)] = ybuf[pl.ds(c * per, per), my_rows, :]
+
+        def give(late):
+            for k, piece in enumerate(pieces[:late]):
+                if c * per <= piece[0] < (c + 1) * per:
+                    for peer in (far, near, side):
+                        back_copy(ybuf, out, sends.at[1], brecv.at[k], share, me_f, peer, piece).start()
+
+        each_job(pieces, give)
+        own_rows(ybuf, out, share, me_f, (c * per, per))
 
     def momentum(group):
         first, last = groups[group]
@@ -220,115 +268,140 @@
         pl.semaphore_wait(ready, nt - 1)
         tell(ready, {"fsdp": side})
 
-    grams(0)
-    factors(0)
-    apply(0)
-    for c in range(1, chunks + 1):
-        if c < chunks:
-            grams(c)
-        if c > 1:
-            apply(c - 1)
-        if c < chunks:
-            factors(c)
+    for act, c in ORDER:
+        (grams, factors, apply)[act](c)
 
     fetch.wait()
-    for c in range(chunks):
-        rows_landed(c, brecv)
-        for peer in range(LINE):
-            here = pl.ds(peer * share + c * per, per)
-            new[here] = wbuf[here] - learn_rate * out[here]
-
+
+    def take(late):
+        for k, piece in enumerate(pieces[:late]):
+            update(new, wbuf, out, brecv.at[k], share, piece)
+        sent(out, sends.at[1], pieces[:late])
+
+    each_job(pieces, take)
     landed(mom.at[pl.ds(0, mats - share)], sends.at[0])
-    landed(mom.at[pl.ds(0, mats - share)], sends.at[1])
     landed(gsend, sends.at[2])
     landed(gsend, sends.at[3])
 
 
-def early_momentum(slopes, moments, mom_out, inputs, held, loads, writes):
-    @pl.when(lax.axis_index("fsdp") == 0)
-    def _():
-        parts = loads.shape[0]
-        some = mom_out.shape[0] // parts
-
-        def part(j):
-            return pl.ds(j * some, some)
-
-        for j in range(parts):
-            pltpu.make_async_copy(slopes.at[part(j)], inputs.at[0, part(j)], loads.at[j]).start()
-            pltpu.make_async_copy(moments.at[part(j)], inputs.at[1, part(j)], loads.at[j]).start()
-        for j in range(parts):
-            arrived = inputs.at[:, part(j)]
-            pltpu.make_async_copy(arrived, arrived, loads.at[j]).wait()
-            held[part(j)] = hold_rate * inputs[1, part(j)] + inputs[0, part(j)]
-            pltpu.make_async_copy(held.at[part(j)], mom_out.at[part(j)], writes).start()
-        pltpu.make_async_copy(held, mom_out, writes).wait()
-
-
-def finish(new, mom, early, new_out, mom_out, sems):
-    late = lax.axis_index("fsdp") > 0
-    rest = pltpu.make_async_copy(mom, mom_out, sems.at[0])
-    pl.when(late)(rest.start)
-    last = pltpu.make_async_copy(new, new_out, sems.at[1])
-    last.start()
-    pl.when(late)(rest.wait)
-    last.wait()
+def last_kernel(chunks, ybuf, wbuf, written, new, out, sends, arrivals):
+    me_f, far, near, side = places()
+    share = ybuf.shape[0]
+    pieces = pieces_of(share, chunks)
+    barrier = pltpu.get_barrier_semaphore()
+    for peer in (near, far, side):
+        tell(barrier, {"fsdp": peer})
+
+    def finish_job(late):
+        pl.semaphore_wait(barrier, LINE - 1)
+        for peer in (far, near, side):
+            for k, piece in enumerate(pieces[late:]):
+                back_copy(ybuf, out, sends, arrivals.at[k], share, me_f, peer, piece).start()
+        for piece in pieces[late:]:
+            own_rows(ybuf, out, share, me_f, piece)
+        for k, piece in enumerate(pieces[late:]):
+            update(new, wbuf, out, arrivals.at[k], share, piece)
+        sent(out, sends, pieces[late:])
+
+    each_job(pieces, finish_job)
+
+
+def copies_of(new, new_out, sems, share, first, last):
+    copies = []
+    for owner in range(LINE):
+        here = pl.ds(owner * share + first, last - first)
+        copies.append(pltpu.make_async_copy(new.at[here], new_out.at[here], sems.at[owner]))
+    return copies
+
+
+def write_first(chunks, new, mom, new_out, mom_out, sems):
+    share = new.shape[0] // LINE
+    pieces = pieces_of(share, chunks)
+
+    def write(late):
+        copies = [pltpu.make_async_copy(mom, mom_out, sems.at[LINE])]
+        copies += copies_of(new, new_out, sems, share, 0, pieces[late][0])
+        for copy in copies:
+            copy.start()
+        for copy in copies:
+            copy.wait()
+
+    each_job(pieces, write)
+
+
+def write_last(chunks, new, written, new_out, sems):
+    share = new.shape[0] // LINE
+    pieces = pieces_of(share, chunks)
+
+    def write(late):
+        copies = copies_of(new, new_out, sems, share, pieces[late][0], share)
+        for copy in copies:
+            copy.start()
+        for copy in copies:
+            copy.wait()
+
+    each_job(pieces, write)
 
 
 def stepped(nf, nt, slopes_in, moments_in, weights_in):
     mats, rows, wide = slopes_in.shape
     side, share = rows * nf, mats // nf
-    most = share // nt
-    chunks = max(k for k in range(1, 5) if most % k == 0)
+    chunks = CHUNKS
     per = share // chunks
     each = per // nt
     vmem, dma, flag = pltpu.VMEM, pltpu.SemaphoreType.DMA, pltpu.SemaphoreType.REGULAR
     shape = jax.ShapeDtypeStruct(slopes_in.shape, jnp.float32)
-    held = [pl.BlockSpec(memory_space=pltpu.VMEM)] * 2
+    whole = jax.ShapeDtypeStruct((share, side, wide), jnp.float32)
+    held = [pl.BlockSpec(memory_space=pltpu.VMEM)]
     far = [pl.BlockSpec(memory_space=pltpu.HBM)]
-    inputs = [pltpu.with_memory_space_constraint(x, pltpu.HBM) for x in (slopes_in, moments_in, weights_in)]
-    early = pl.pallas_call(
-        early_momentum,
-        out_shape=shape,
-        in_specs=far * 2,
-        out_specs=far[0],
+    new, mom, results, weights = pl.pallas_call(
+        functools.partial(kernel, nt, chunks),
+        out_shape=[shape, shape, whole, shape],
+        in_specs=far * 3,
+        out_specs=held * 4,
         scratch_shapes=[
-            vmem((2,) + slopes_in.shape, jnp.float32),
-            vmem(slopes_in.shape, jnp.float32),
-            dma((max(k for k in range(1, 5) if mats % k == 0),)), dma,
-        ],
-        compiler_params=pltpu.CompilerParams(vmem_limit_bytes=16 * 2**20),
-    )(*inputs[:2])
-    early = pltpu.with_memory_space_constraint(early, pltpu.HBM)
-    new, mom = pl.pallas_call(
-        functools.partial(kernel, nt, chunks),
-        out_shape=[shape] * 2,
-        in_specs=far * 4,
-        out_specs=held,
-        scratch_shapes=[
-            vmem(slopes_in.shape, jnp.float32),
             vmem(slopes_in.shape, jnp.float32),
             vmem((2,) + slopes_in.shape, jnp.float32),
             vmem((share, side, wide), jnp.float32),
             vmem((chunks, nt - 1, each, side, side), jnp.float32),
             vmem((chunks, nt, each, side, side), jnp.float32),
             vmem((chunks, nt, each, side, side), jnp.float32),
-            vmem((share, side, wide), jnp.float32),
             dma((4,)), dma((chunks,)), dma((chunks,)), dma((chunks,)), dma((chunks,)),
             dma((5,)), flag, flag,
         ],
         compiler_params=pltpu.CompilerParams(
             collective_id=0, has_side_effects=True, vmem_limit_bytes=32 * 2**20
         ),
-    )(*inputs, early)
-    return pl.pallas_call(
-        finish,
+    )(*(pltpu.with_memory_space_constraint(x, pltpu.HBM) for x in (slopes_in, moments_in, weights_in)))
+    new_out, mom_out = pl.pallas_call(
+        functools.partial(write_first, chunks),
         out_shape=[shape] * 2,
+        in_specs=held * 2,
+        out_specs=far * 2,
+        scratch_shapes=[dma((LINE + 1,))],
+        compiler_params=pltpu.CompilerParams(vmem_limit_bytes=2**20),
+    )(new, mom)
+    new_out = pltpu.with_memory_space_constraint(new_out, pltpu.HBM)
+    last = pl.pallas_call(
+        functools.partial(last_kernel, chunks),
+        out_shape=shape,
+        in_specs=held * 2 + far,
+        out_specs=held[0],
+        scratch_shapes=[vmem(slopes_in.shape, jnp.float32), dma, dma((max(LATE_CHUNKS),))],
+        compiler_params=pltpu.CompilerParams(
+            collective_id=1, has_side_effects=True, vmem_limit_bytes=4 * 2**20
+        ),
+    )(results, weights, new_out)
+    new_out = pl.pallas_call(
+        functools.partial(write_last, chunks),
+        out_shape=shape,
         in_specs=held + far,
-        out_specs=far * 2,
-        input_output_aliases={2: 1},
-        scratch_shapes=[dma((2,))],
+        out_specs=far[0],
+        input_output_aliases={1: 0},
+        scratch_shapes=[dma((LINE,))],
         compiler_params=pltpu.CompilerParams(vmem_limit_bytes=2**20),
-    )(new, mom, early)
+    )(last, new_out)
+    return new_out, mom_out
 
 
 def orthogonal_plain(new_momentum):
@@ -342,7 +415,8 @@
 
 def body(nf, nt, slopes_in, moments_in, weights_in):
     rows, wide = slopes_in.shape[1:]
-    if nf == LINE and nt > 1 and rows % 8 == 0 and wide % 128 == 0:
+    share = slopes_in.shape[0] // nf
+    if nf == LINE and nt > 1 and share % (CHUNKS * nt) == 0 and rows % 8 == 0 and wide % 128 == 0:
         return stepped(nf, nt, slopes_in, moments_in, weights_in)
     new_momentum = hold_rate * moments_in + slopes_in
     new_weights = weights_in - learn_rate * orthogonal_plain(new_momentum)

time: 96.6 us -> 95.6 us (0.990)
    pallas_call x3 -> x4, Pallas kernels: 95.5 us -> 94.6 us  [the longest x1 70.9 us: stepped(): pl.pallas_call(functools.partial(kernel, nt, chunks), out_shape=[shape, s...]
where the time goes in v3:
time: 95.6 us; the launch traced here: 95.3 us
  Pallas kernels  94.6 us (99%)
    pallas_call x1, Pallas kernels, stepped(): pl.pallas_call(functools.partial(kernel, nt, chunks), out_shape=[shape, s...  70.9 us
    pallas_call x1, Pallas kernels, stepped(): pl.pallas_call(functools.partial(last_kernel, chunks), out_shape=shape, i...  21 us

profile of v3, /device:TPU:15, one launch (start us, length us, event | category | flops | bytes accessed | tf_op | source)
XLA Modules:
  0.0 95.3 jit_solution(4354951052601479106)
XLA Ops:
  0.6 70.9 %shard_map.50 = (f32[64,32,256]{2,1,0:T(8,128)S(1)}, f32[64,32,256]{2,1,0:T(8,128)S(1)}, f32[16,128,256]{2,1,0:T(8,128)S(1)}, f32[64,32,256]{2,1,0:T(8,128)S(1)}) custom-call(f32[64,32,256]{2,1,0:T(8,128)} %slopes.1, f32[64,32,256]{2,1,0:T(8,128)} %moments.1, f32[64,32,256]{2,1,0:T(8,128)} %weights.1), custom_call_target="tpu_custom_call" | custom-call | tf_op jit(solution)/shard_map/pallas_call | solution.py:357
  71.5 1.7 %shard_map.51 = (f32[64,32,256]{2,1,0:T(8,128)}, f32[64,32,256]{2,1,0:T(8,128)}) custom-call(f32[64,32,256]{2,1,0:T(8,128)S(1)} %get-tuple-element.10.new, f32[64,32,256]{2,1,0:T(8,128)S(1)} %get-tuple-element.11.mom), custom_call_target="tpu_custom_call" | custom-call | tf_op jit(solution)/shard_map/pallas_call | solution.py:376
  73.2 21.0 %shard_map.52.new = f32[64,32,256]{2,1,0:T(8,128)S(1)} custom-call(f32[16,128,256]{2,1,0:T(8,128)S(1)} %get-tuple-element.8.ybuf, f32[64,32,256]{2,1,0:T(8,128)S(1)} %get-tuple-element.9.wbuf, f32[64,32,256]{2,1,0:T(8,128)} %get-tuple-element.12.written), custom_call_target="tpu_custom_call" | custom-call | tf_op jit(solution)/shard_map/pallas_call | solution.py:385
  94.3 1.0 %shard_map.53 = f32[64,32,256]{2,1,0:T(8,128)} custom-call(f32[64,32,256]{2,1,0:T(8,128)S(1)} %shard_map.52.new, f32[64,32,256]{2,1,0:T(8,128)} %get-tuple-element.12.written), custom_call_target="tpu_custom_call", output_to_operand_aliasing={{}: (1, {})} | custom-call | tf_op jit(solution)/shard_map/pallas_call | solution.py:395

commit v4 on v3

--- a/solution.py
+++ b/solution.py
@@ -10,7 +10,7 @@
 ITERS = 5
 LINE = 4
 AHEAD = 2
-LATE_CHUNKS = (1, 2)
+LATE_CHUNKS = (0, 2)
 CHUNKS = 4
 ORDER = ((0, 0), (1, 0), (2, 0), (0, 1), (1, 1), (0, 2), (2, 1), (1, 2), (0, 3), (1, 3), (2, 2), (2, 3))
 
@@ -289,10 +289,12 @@
     share = ybuf.shape[0]
     pieces = pieces_of(share, chunks)
     barrier = pltpu.get_barrier_semaphore()
-    for peer in (near, far, side):
-        tell(barrier, {"fsdp": peer})
 
     def finish_job(late):
+        if late == len(pieces):
+            return
+        for peer in (near, far, side):
+            tell(barrier, {"fsdp": peer})
         pl.semaphore_wait(barrier, LINE - 1)
         for peer in (far, near, side):
             for k, piece in enumerate(pieces[late:]):
@@ -306,10 +308,10 @@
     each_job(pieces, finish_job)
 
 
-def copies_of(new, new_out, sems, share, first, last):
+def copies_of(new, new_out, sems, share, pieces):
     copies = []
-    for owner in range(LINE):
-        here = pl.ds(owner * share + first, last - first)
+    for owner in range(LINE if pieces else 0):
+        here = pl.ds(owner * share + pieces[0][0], sum(size for _, size in pieces))
         copies.append(pltpu.make_async_copy(new.at[here], new_out.at[here], sems.at[owner]))
     return copies
 
@@ -320,7 +322,7 @@
 
     def write(late):
         copies = [pltpu.make_async_copy(mom, mom_out, sems.at[LINE])]
-        copies += copies_of(new, new_out, sems, share, 0, pieces[late][0])
+        copies += copies_of(new, new_out, sems, share, pieces[:late])
         for copy in copies:
             copy.start()
         for copy in copies:
@@ -334,7 +336,7 @@
     pieces = pieces_of(share, chunks)
 
     def write(late):
-        copies = copies_of(new, new_out, sems, share, pieces[late][0], share)
+        copies = copies_of(new, new_out, sems, share, pieces[late:])
         for copy in copies:
             copy.start()
         for copy in copies:

time: 95.6 us -> 95.2 us (level)
  no operation moved by 1% of the time
where the time goes in v4:
time: 95.2 us; the launch traced here: 95.1 us
  Pallas kernels  94.4 us (99%)
    pallas_call x1, Pallas kernels, stepped(): pl.pallas_call(functools.partial(kernel, nt, chunks), out_shape=[shape, s...  70.9 us
    pallas_call x1, Pallas kernels, stepped(): pl.pallas_call(functools.partial(last_kernel, chunks), out_shape=shape, i...  20.8 us

profile of v4, /device:TPU:15, one launch (start us, length us, event | category | flops | bytes accessed | tf_op | source)
XLA Modules:
  0.0 95.1 jit_solution(5116729592482283131)
XLA Ops:
  0.6 70.9 %shard_map.50 = (f32[64,32,256]{2,1,0:T(8,128)S(1)}, f32[64,32,256]{2,1,0:T(8,128)S(1)}, f32[16,128,256]{2,1,0:T(8,128)S(1)}, f32[64,32,256]{2,1,0:T(8,128)S(1)}) custom-call(f32[64,32,256]{2,1,0:T(8,128)} %slopes.1, f32[64,32,256]{2,1,0:T(8,128)} %moments.1, f32[64,32,256]{2,1,0:T(8,128)} %weights.1), custom_call_target="tpu_custom_call" | custom-call | tf_op jit(solution)/shard_map/pallas_call | solution.py:359
  71.5 1.7 %shard_map.51 = (f32[64,32,256]{2,1,0:T(8,128)}, f32[64,32,256]{2,1,0:T(8,128)}) custom-call(f32[64,32,256]{2,1,0:T(8,128)S(1)} %get-tuple-element.10.new, f32[64,32,256]{2,1,0:T(8,128)S(1)} %get-tuple-element.11.mom), custom_call_target="tpu_custom_call" | custom-call | tf_op jit(solution)/shard_map/pallas_call | solution.py:378
  73.2 20.8 %shard_map.52.new = f32[64,32,256]{2,1,0:T(8,128)S(1)} custom-call(f32[16,128,256]{2,1,0:T(8,128)S(1)} %get-tuple-element.8.ybuf, f32[64,32,256]{2,1,0:T(8,128)S(1)} %get-tuple-element.9.wbuf, f32[64,32,256]{2,1,0:T(8,128)} %get-tuple-element.12.written), custom_call_target="tpu_custom_call" | custom-call | tf_op jit(solution)/shard_map/pallas_call | solution.py:387
  94.1 1.0 %shard_map.53 = f32[64,32,256]{2,1,0:T(8,128)} custom-call(f32[64,32,256]{2,1,0:T(8,128)S(1)} %shard_map.52.new, f32[64,32,256]{2,1,0:T(8,128)} %get-tuple-element.12.written), custom_call_target="tpu_custom_call", output_to_operand_aliasing={{}: (1, {})} | custom-call | tf_op jit(solution)/shard_map/pallas_call | solution.py:397

commit v5 on v4

--- a/solution.py
+++ b/solution.py
@@ -10,7 +10,7 @@
 ITERS = 5
 LINE = 4
 AHEAD = 2
-LATE_CHUNKS = (0, 2)
+LATE_PIECES = ((0, 0), (2, 2))
 CHUNKS = 4
 ORDER = ((0, 0), (1, 0), (2, 0), (0, 1), (1, 1), (0, 2), (2, 1), (1, 2), (0, 3), (1, 3), (2, 2), (2, 3))
 
@@ -67,13 +67,22 @@
 
 def pieces_of(share, chunks):
     per = share // chunks
-    return [(c * per, per) for c in range(chunks)]
+    first = share - 2 * per
+    whole = [(c * per, per) for c in range(chunks)]
+    return whole[:-2] + [(first, per // 2), (first + per // 2, per - per // 2)] + whole[-1:]
 
 
 def each_job(pieces, act):
     kind = lax.rem(lax.axis_index("job"), 2)
-    for number, late in enumerate(LATE_CHUNKS):
-        pl.when(kind == number)(functools.partial(act, len(pieces) - late))
+    me_f = lax.axis_index("fsdp")
+    place = me_f * (3 - me_f)
+    for number, late in enumerate(LATE_PIECES):
+        ends, inside = (len(pieces) - few for few in late)
+        if ends == inside:
+            pl.when(kind == number)(functools.partial(act, ends, ends, ends, ends))
+        else:
+            pl.when((kind == number) & (place > 0))(functools.partial(act, ends, inside, ends, inside))
+            pl.when((kind == number) & (place == 0))(functools.partial(act, ends, inside, inside, ends))
 
 
 def back_copy(ybuf, out, sends, arrivals, share, me_f, peer, piece):
@@ -103,9 +112,9 @@
         new[here] = wbuf[here] - learn_rate * out[here]
 
 
-def sent(out, sends, pieces):
-    total = sum(size for _, size in pieces)
-    landed(out.at[pl.ds(0, (LINE - 1) * total)], sends)
+def sent(out, sends, groups):
+    total = sum(size for pieces in groups for _, size in pieces)
+    landed(out.at[pl.ds(0, total)], sends)
 
 
 def kernel(nt, chunks, slopes, moments, weights, new, mom, ybuf, wbuf, out, inputs, xbuf, gsend, grecv, qrecv, sends, frecv, gr, qr, brecv, loads, hello, ready):
@@ -205,10 +214,10 @@
             for e in range(each):
                 ybuf[first + e] = dot(qrecv[c, d, e], xbuf[first + e])
 
-        def give(late):
-            for k, piece in enumerate(pieces[:late]):
-                if c * per <= piece[0] < (c + 1) * per:
-                    for peer in (far, near, side):
+        def give(*cuts):
+            for peer, cut in zip((far, near, side), cuts):
+                for k, piece in enumerate(pieces[:cut]):
+                    if piece[0] // per == c:
                         back_copy(ybuf, out, sends.at[1], brecv.at[k], share, me_f, peer, piece).start()
 
         each_job(pieces, give)
@@ -273,10 +282,10 @@
 
     fetch.wait()
 
-    def take(late):
-        for k, piece in enumerate(pieces[:late]):
+    def take(*cuts):
+        for k, piece in enumerate(pieces[:cuts[-1]]):
             update(new, wbuf, out, brecv.at[k], share, piece)
-        sent(out, sends.at[1], pieces[:late])
+        sent(out, sends.at[1], [pieces[:cut] for cut in cuts[:-1]])
 
     each_job(pieces, take)
     landed(mom.at[pl.ds(0, mats - share)], sends.at[0])
@@ -290,20 +299,21 @@
     pieces = pieces_of(share, chunks)
     barrier = pltpu.get_barrier_semaphore()
 
-    def finish_job(late):
-        if late == len(pieces):
+    def finish_job(*cuts):
+        if min(cuts) == len(pieces):
             return
         for peer in (near, far, side):
             tell(barrier, {"fsdp": peer})
         pl.semaphore_wait(barrier, LINE - 1)
-        for peer in (far, near, side):
-            for k, piece in enumerate(pieces[late:]):
+        for peer, cut in zip((far, near, side), cuts):
+            for k, piece in list(enumerate(pieces))[cut:]:
                 back_copy(ybuf, out, sends, arrivals.at[k], share, me_f, peer, piece).start()
-        for piece in pieces[late:]:
+        mine = list(enumerate(pieces))[cuts[-1]:]
+        for _, piece in mine:
             own_rows(ybuf, out, share, me_f, piece)
-        for k, piece in enumerate(pieces[late:]):
+        for k, piece in mine:
             update(new, wbuf, out, arrivals.at[k], share, piece)
-        sent(out, sends, pieces[late:])
+        sent(out, sends, [pieces[cut:] for cut in cuts[:-1]])
 
     each_job(pieces, finish_job)
 
@@ -320,9 +330,9 @@
     share = new.shape[0] // LINE
     pieces = pieces_of(share, chunks)
 
-    def write(late):
+    def write(*cuts):
         copies = [pltpu.make_async_copy(mom, mom_out, sems.at[LINE])]
-        copies += copies_of(new, new_out, sems, share, pieces[:late])
+        copies += copies_of(new, new_out, sems, share, pieces[:cuts[-1]])
         for copy in copies:
             copy.start()
         for copy in copies:
@@ -335,8 +345,8 @@
     share = new.shape[0] // LINE
     pieces = pieces_of(share, chunks)
 
-    def write(late):
-        copies = copies_of(new, new_out, sems, share, pieces[late:])
+    def write(*cuts):
+        copies = copies_of(new, new_out, sems, share, pieces[cuts[-1]:])
         for copy in copies:
             copy.start()
         for copy in copies:
@@ -368,7 +378,7 @@
             vmem((chunks, nt - 1, each, side, side), jnp.float32),
             vmem((chunks, nt, each, side, side), jnp.float32),
             vmem((chunks, nt, each, side, side), jnp.float32),
-            dma((4,)), dma((chunks,)), dma((chunks,)), dma((chunks,)), dma((chunks,)),
+            dma((4,)), dma((chunks,)), dma((chunks,)), dma((chunks,)), dma((chunks + 1,)),
             dma((5,)), flag, flag,
         ],
         compiler_params=pltpu.CompilerParams(
@@ -389,7 +399,7 @@
         out_shape=shape,
         in_specs=held * 2 + far,
         out_specs=held[0],
-        scratch_shapes=[vmem(slopes_in.shape, jnp.float32), dma, dma((max(LATE_CHUNKS),))],
+        scratch_shapes=[vmem(slopes_in.shape, jnp.float32), dma, dma((chunks + 1,))],
         compiler_params=pltpu.CompilerParams(
             collective_id=1, has_side_effects=True, vmem_limit_bytes=4 * 2**20
         ),
@@ -418,7 +428,7 @@
 def body(nf, nt, slopes_in, moments_in, weights_in):
     rows, wide = slopes_in.shape[1:]
     share = slopes_in.shape[0] // nf
-    if nf == LINE and nt > 1 and share % (CHUNKS * nt) == 0 and rows % 8 == 0 and wide % 128 == 0:
+    if nf == LINE and nt > 1 and share % (CHUNKS * nt) == 0 and share // CHUNKS > 1 and rows % 8 == 0 and wide % 128 == 0:
         return stepped(nf, nt, slopes_in, moments_in, weights_in)
     new_momentum = hold_rate * moments_in + slopes_in
     new_weights = weights_in - learn_rate * orthogonal_plain(new_momentum)

time: 95.2 us -> 95.1 us (level)
    pallas_call x1, Pallas kernels: 20.8 us -> 13 us  [stepped(): pl.pallas_call(functools.partial(last_kernel, chunks), out_shape=shape, i...]
    pallas_call x1, Pallas kernels: 70.9 us -> 78.6 us  [stepped(): pl.pallas_call(functools.partial(kernel, nt, chunks), out_shape=[shape, s...]
where the time goes in v5:
time: 95.1 us; the launch traced here: 95 us
  Pallas kernels  94.3 us (99%)
    pallas_call x1, Pallas kernels, stepped(): pl.pallas_call(functools.partial(kernel, nt, chunks), out_shape=[shape, s...  78.6 us
    pallas_call x1, Pallas kernels, stepped(): pl.pallas_call(functools.partial(last_kernel, chunks), out_shape=shape, i...  13 us

profile of v5, /device:TPU:15, one launch (start us, length us, event | category | flops | bytes accessed | tf_op | source)
XLA Modules:
  0.0 95.0 jit_solution(12172650376056185282)
XLA Ops:
  0.6 78.6 %shard_map.50 = (f32[64,32,256]{2,1,0:T(8,128)S(1)}, f32[64,32,256]{2,1,0:T(8,128)S(1)}, f32[16,128,256]{2,1,0:T(8,128)S(1)}, f32[64,32,256]{2,1,0:T(8,128)S(1)}) custom-call(f32[64,32,256]{2,1,0:T(8,128)} %slopes.1, f32[64,32,256]{2,1,0:T(8,128)} %moments.1, f32[64,32,256]{2,1,0:T(8,128)} %weights.1), custom_call_target="tpu_custom_call" | custom-call | tf_op jit(solution)/shard_map/pallas_call | solution.py:369
  79.3 1.8 %shard_map.51 = (f32[64,32,256]{2,1,0:T(8,128)}, f32[64,32,256]{2,1,0:T(8,128)}) custom-call(f32[64,32,256]{2,1,0:T(8,128)S(1)} %get-tuple-element.10.new, f32[64,32,256]{2,1,0:T(8,128)S(1)} %get-tuple-element.11.mom), custom_call_target="tpu_custom_call" | custom-call | tf_op jit(solution)/shard_map/pallas_call | solution.py:388
  81.1 13.0 %shard_map.52.new = f32[64,32,256]{2,1,0:T(8,128)S(1)} custom-call(f32[16,128,256]{2,1,0:T(8,128)S(1)} %get-tuple-element.8.ybuf, f32[64,32,256]{2,1,0:T(8,128)S(1)} %get-tuple-element.9.wbuf, f32[64,32,256]{2,1,0:T(8,128)} %get-tuple-element.12.written), custom_call_target="tpu_custom_call" | custom-call | tf_op jit(solution)/shard_map/pallas_call | solution.py:397
  94.0 0.9 shard_map.53

commit v6 on v5

--- a/solution.py
+++ b/solution.py
@@ -271,7 +271,7 @@
                 there(c, peer).start()
         pl.semaphore_wait(hello, 1)
         for c in range(chunks):
-            for peer in (near, far, side) if c >= AHEAD else (far,):
+            for peer in (far, near, side) if c >= AHEAD else (far,):
                 there(c, peer).start()
         tell_tp(ready)
         pl.semaphore_wait(ready, nt - 1)

time: 95.1 us -> 95.1 us (level)
  no operation moved by 1% of the time
where the time goes in v6:
time: 95.1 us; the launch traced here: 94.9 us
  Pallas kernels  94.3 us (99%)
    pallas_call x1, Pallas kernels, stepped(): pl.pallas_call(functools.partial(kernel, nt, chunks), out_shape=[shape, s...  78.6 us
    pallas_call x1, Pallas kernels, stepped(): pl.pallas_call(functools.partial(last_kernel, chunks), out_shape=shape, i...  13 us

profile of v6, /device:TPU:15, one launch (start us, length us, event | category | flops | bytes accessed | tf_op | source)
XLA Modules:
  0.0 94.9 jit_solution(70183679047552601)
XLA Ops:
  0.6 78.6 %shard_map.50 = (f32[64,32,256]{2,1,0:T(8,128)S(1)}, f32[64,32,256]{2,1,0:T(8,128)S(1)}, f32[16,128,256]{2,1,0:T(8,128)S(1)}, f32[64,32,256]{2,1,0:T(8,128)S(1)}) custom-call(f32[64,32,256]{2,1,0:T(8,128)} %slopes.1, f32[64,32,256]{2,1,0:T(8,128)} %moments.1, f32[64,32,256]{2,1,0:T(8,128)} %weights.1), custom_call_target="tpu_custom_call" | custom-call | tf_op jit(solution)/shard_map/pallas_call | solution.py:369
  79.2 1.8 %shard_map.51 = (f32[64,32,256]{2,1,0:T(8,128)}, f32[64,32,256]{2,1,0:T(8,128)}) custom-call(f32[64,32,256]{2,1,0:T(8,128)S(1)} %get-tuple-element.10.new, f32[64,32,256]{2,1,0:T(8,128)S(1)} %get-tuple-element.11.mom), custom_call_target="tpu_custom_call" | custom-call | tf_op jit(solution)/shard_map/pallas_call | solution.py:388
  81.0 13.0 %shard_map.52.new = f32[64,32,256]{2,1,0:T(8,128)S(1)} custom-call(f32[16,128,256]{2,1,0:T(8,128)S(1)} %get-tuple-element.8.ybuf, f32[64,32,256]{2,1,0:T(8,128)S(1)} %get-tuple-element.9.wbuf, f32[64,32,256]{2,1,0:T(8,128)} %get-tuple-element.12.written), custom_call_target="tpu_custom_call" | custom-call | tf_op jit(solution)/shard_map/pallas_call | solution.py:397
  94.0 0.9 shard_map.53
